TPU v7x, 512 devices: a whole 4x8x8 slice. The times are simulated.
512 devices in a mesh: row: 32 (over z, x), col: 16 (over y, core).
Axes of the slice: x: 4, y: 8, z: 8, core: 2. Of those that a mesh axis runs over, the one named last changes fastest.
Arguments:
- lower: bfloat16 [32, 3, 512, 2, 512], P('row', None, None, None, 'col'), as said below
- rhs: bfloat16 [32, 3, 512, 8192], P('row', None, None, 'col'), may hold values from -6 to 6
- tile_map: int32 [16], replicated, may hold values from 0 to 15, each once
Outputs:
- overwritten: bfloat16 [32, 3, 512, 8192], P('row', None, None, 'col')
Inputs may be any that keep to these rules, and one draw needn't show every extreme that they name: tile_map is a permutation of 0 to 15. lower[0, 0, :, 0, :] and lower[1, 0, :, 1, :] are lower triangular with diagonal entries between 2 and 3; lower[0, 0, :, 1, :] is zero.
All inputs are finite; a program needn't handle non-finite values.
Results may differ from a plain program's by a relative error of at most 0.0032.
Values may be sent and summed in bfloat16 or wider, within the bound.
A program may use at most 64 MiB of HBM per device.

v0:
```python
import jax
import jax.numpy as jnp
from jax import lax
from jax.sharding import Mesh
from jax.sharding import PartitionSpec as P

ROW = ("row_0", "row_1")


def spread(shard, axes, root):
    shard = jnp.where(lax.axis_index(axes) == root, shard, jnp.zeros_like(shard))
    for axis in axes:
        shard = lax.psum(shard, axis)
    return shard


def reorder(block, tile_map, tile):
    shape = block.shape
    tiles = block.reshape(shape[:-1] + (shape[-1] // tile, tile))
    return jnp.take(tiles, tile_map, axis=3).reshape(shape)


def body(lower, rhs, tile_map):
    tile = lower.shape[2]
    here = lax.axis_index(ROW)
    whole = lax.all_gather(lower, "col", axis=4, tiled=True)
    panels = whole[0]
    rows = panels.shape[0] * tile
    rhs = lax.all_to_all(
        reorder(
            lax.all_to_all(rhs, "col", split_axis=2, concat_axis=3, tiled=True), tile_map, tile
        ),
        "col",
        split_axis=3,
        concat_axis=2,
        tiled=True,
    )
    work = rhs[0].astype(jnp.float32)
    identity = jnp.eye(tile, dtype=jnp.float32)
    solved_rows = []
    for panel in range(2):
        mine = jnp.where(
            here == panel, jnp.tril(panels[0, :, panel, :].astype(jnp.float32)), identity
        )
        local = jax.scipy.linalg.solve_triangular(mine, work[0], lower=True).astype(jnp.bfloat16)
        solved = spread(local, ROW, panel)
        flat = panels[:, :, panel, :].reshape(rows, tile)
        work = work - jnp.dot(flat, solved, preferred_element_type=jnp.float32).reshape(work.shape)
        solved_rows.append(solved)
    first, second = (solved_rows[0], solved_rows[1])
    result = work.astype(jnp.bfloat16)
    leading = jnp.where(here == 0, first, jnp.where(here == 1, second, result[0]))
    result = result.at[0].set(leading)[None]
    return result


def solution(mesh):
    torus = Mesh(mesh.devices.reshape(8, 4, mesh.shape["col"]), ("row_0", "row_1", "col"))
    return jax.shard_map(
        body,
        mesh=torus,
        in_specs=(P(ROW, None, None, None, "col"), P(ROW, None, None, "col"), P()),
        out_specs=P(ROW, None, None, "col"),
        check_vma=False,
    )
```

profile of v0, /device:TPU:8, one launch (start us, length us, event | category | flops | bytes accessed | tf_op | source)
XLA Modules:
  0.0 522.2 jit_solution(17489380718761430764)
XLA Ops:
  6.5 4.1 copy.38
  10.6 9.4 %all-to-all-start = ((bf16[1,3,512,512]{3,1,0,2:T(4,128)(2,1)}), bf16[1,3,512,512]{3,1,0,2:T(4,128)(2,1)S(1)}, u32[]{:S(2)}, u32[]{:S(2)}) async-start(bf16[1,3,512,512]{3,1,0,2:T(4,128)(2,1)} %copy.38), calls=%async_computation | async-start | bytes 4194304 | tf_op jit(solution)/shard_map/all_to_all | solution.py:31
  20.1 0.9 copy.44
  21.2 56.9 %all-to-all-done = bf16[1,3,512,512]{3,1,0,2:T(4,128)(2,1)S(1)} async-done(((bf16[1,3,512,512]{3,1,0,2:T(4,128)(2,1)}), bf16[1,3,512,512]{3,1,0,2:T(4,128)(2,1)S(1)}, u32[]{:S(2)}, u32[]{:S(2)}) %all-to-all-start) | async-done | bytes 1572896 | tf_op jit(solution)/shard_map/all_to_all | solution.py:31
  78.1 1.5 copy.39
  79.6 2.1 gather_fusion
  81.6 0.9 copy.40
  82.5 0.8 gather.9
  83.5 8.3 %copy.41 = bf16[1,3,32,8192]{2,1,0,3:T(4,128)(2,1)} copy(bf16[1,3,32,8192]{3,2,1,0:T(8,128)(2,1)S(1)} %broadcast_select_fusion) | data formatting | bytes 3145728 | tf_op jit(solution)/shard_map/jit(_take)/select_n | solution.py:20
  91.8 13.2 %reshape.163 = bf16[16,2,24576]{2,1,0:T(2,128)(2,1)} reshape(bf16[8192,1,3,32]{3,2,1,0:T(4,128)(2,1)} %bitcast.122) | data formatting | bytes 3145728
  105.0 8.1 %all-to-all-start.1 = ((bf16[16,2,24576]{2,1,0:T(2,128)(2,1)}), bf16[16,2,24576]{2,1,0:T(2,128)(2,1)}, u32[]{:S(2)}, u32[]{:S(2)}) async-start(bf16[16,2,24576]{2,1,0:T(2,128)(2,1)} %reshape.163), calls=%async_computation.1 | async-start | bytes 3145728 | tf_op jit(solution)/shard_map/all_to_all | solution.py:29
  113.4 7.0 %copy.45 = bf16[1,3,512,2,512]{4,2,3,1,0:T(8,128)(2,1)S(1)} copy(bf16[1,3,512,2,512]{2,3,1,0,4:T(2,128)(2,1)} %all-gather.2.cloned.1.call-done) | data formatting | bytes 6291456 | tf_op jit(solution)/shard_map/all_gather | solution.py:26
  120.5 1.8 fusion.3
  122.7 11.5 %while.5 = (s32[]{:T(128)}, f32[512,512]{1,0:T(8,128)}, s32[4,2]{0,1:T(2,128)S(1)}, f32[4,128,128]{2,1,0:T(8,128)S(1)}, s32[]{:T(128)}) while((s32[]{:T(128)}, f32[512,512]{1,0:T(8,128)}, s32[4,2]{0,1:T(2,128)S(1)}, f32[4,128,128]{2,1,0:T(8,128)S(1)}, s32[]{:T(128)}) %tuple.41), condition=%wide.while_cond.1, body=%wide.while_body.1.sunk | while | flops 2 | bytes 131189 | solution.py:45
  123.4 2.3 bitcast_dynamic-update-slice_fusion.4
  126.3 2.3 bitcast_dynamic-update-slice_fusion.4
  129.2 2.3 bitcast_dynamic-update-slice_fusion.4
  132.1 2.2 bitcast_dynamic-update-slice_fusion.4
  134.3 39.3 %custom-call.4 = f32[4,128,128]{1,2,0:T(8,128)S(1)} custom-call(f32[4,128,128]{2,1,0:T(8,128)S(1)} %get-tuple-element.32), custom_call_target="InvertDiagBlocksLowerTriangular" | custom-call | tf_op jit(solution)/shard_map/jit(_solve_triangular)/triangular_solve | solution.py:45
  173.6 12.6 %reshape.164 = bf16[8192,1,3,32]{3,2,1,0:T(4,128)(2,1)} reshape(bf16[16,2,24576]{2,1,0:T(2,128)(2,1)} %all-to-all-done.1) | data formatting | bytes 3145728
  186.2 9.7 %copy.42 = bf16[1,3,32,8192]{3,2,1,0:T(8,128)(2,1)S(1)} copy(bf16[1,3,32,8192]{2,1,0,3:T(4,128)(2,1)} %bitcast.123) | data formatting | bytes 3145728 | tf_op jit(solution)/shard_map/all_to_all | solution.py:29
  197.2 0.9 copy-done.1
  198.5 1.2 convolution_subtract_fusion.3
  200.2 1.3 convolution_subtract_fusion.2
  202.0 1.6 convolution_subtract_fusion.5
  203.9 0.9 fusion.16
  204.9 83.1 %all-reduce.5.cloned.1.call-done = bf16[512,512]{1,0:T(8,128)(2,1)} async-done(((bf16[512,512]{1,0:T(8,128)(2,1)}), bf16[512,512]{1,0:T(8,128)(2,1)}) %all-reduce.5.cloned.1.call-update) | async-done | bytes 524304 | tf_op jit(solution)/shard_map/psum | solution.py:13
  289.0 13.6 %while.6 = (s32[]{:T(128)}, f32[512,512]{1,0:T(8,128)}, s32[4,2]{0,1:T(2,128)S(1)}, f32[4,128,128]{2,1,0:T(8,128)}, s32[]{:T(128)}) while((s32[]{:T(128)}, f32[512,512]{1,0:T(8,128)}, s32[4,2]{0,1:T(2,128)S(1)}, f32[4,128,128]{2,1,0:T(8,128)}, s32[]{:T(128)}) %tuple.57), condition=%wide.while_cond.1.clone, body=%wide.while_body.1.clone.sunk | while | flops 2 | bytes 132205 | solution.py:45
  289.6 2.8 bitcast_dynamic-update-slice_fusion.5
  293.0 2.8 bitcast_dynamic-update-slice_fusion.5
  296.4 2.8 bitcast_dynamic-update-slice_fusion.5
  299.8 2.7 bitcast_dynamic-update-slice_fusion.5
  302.6 3.7 copy.43
  306.3 40.1 %custom-call.5 = f32[4,128,128]{1,2,0:T(8,128)S(1)} custom-call(f32[4,128,128]{2,1,0:T(8,128)} %get-tuple-element.33), custom_call_target="InvertDiagBlocksLowerTriangular" | custom-call | tf_op jit(solution)/shard_map/jit(_solve_triangular)/triangular_solve | solution.py:45
  346.4 4.0 fusion.50
  350.4 4.3 convolution_bitcast_fusion.1
  354.7 3.6 copy.47
  358.2 2.6 sub.25
  361.4 1.3 convolution_subtract_fusion.1
  363.1 1.3 convolution_subtract_fusion
  364.9 1.6 convolution_subtract_fusion.4
  366.9 0.9 fusion.15
  368.1 77.8 %all-reduce.9.cloned.1.call-done = bf16[512,512]{1,0:T(8,128)(2,1)} async-done(((bf16[512,512]{1,0:T(8,128)(2,1)}), bf16[512,512]{1,0:T(8,128)(2,1)}) %all-reduce.9.cloned.1.call-update) | async-done | bytes 524304 | tf_op jit(solution)/shard_map/psum | solution.py:13
  445.9 54.0 %all-reduce.11.cloned.1.call-done = bf16[512,512]{1,0:T(8,128)(2,1)} async-done(((bf16[512,512]{1,0:T(8,128)(2,1)}), bf16[512,512]{1,0:T(8,128)(2,1)}) %all-reduce.11.cloned.1.call-update) | async-done | bytes 524304 | tf_op jit(solution)/shard_map/psum | solution.py:13
  499.9 4.3 convolution_bitcast_fusion
  504.2 3.6 copy.50
  507.8 5.2 fusion.1
  513.0 2.7 fusion.21
  (64 shorter events, 12.0 us)
Async XLA Ops:
  10.6 9.5 %copy-start.5 = (bf16[1,3,512,2,32]{2,4,3,1,0:T(8,128)(2,1)S(1)}, bf16[1,3,512,2,32]{2,4,3,1,0:T(8,128)(2,1)}, u32[]{:S(2)}) copy-start(bf16[1,3,512,2,32]{2,4,3,1,0:T(8,128)(2,1)} %param.7) | copy-start | bytes 589828
  10.6 10.4 %copy-start.6 = (s32[16]{0:T(128)S(1)}, s32[16]{0:T(128)}, u32[]{:S(2)}) copy-start(s32[16]{0:T(128)} %param.9) | copy-start | bytes 196
  10.6 67.4 %all-to-all-start = ((bf16[1,3,512,512]{3,1,0,2:T(4,128)(2,1)}), bf16[1,3,512,512]{3,1,0,2:T(4,128)(2,1)S(1)}, u32[]{:S(2)}, u32[]{:S(2)}) async-start(bf16[1,3,512,512]{3,1,0,2:T(4,128)(2,1)} %copy.38), calls=%async_computation | async-start | bytes 4194304 | tf_op jit(solution)/shard_map/all_to_all | solution.py:31
  20.1 93.4 %all-gather.2.cloned.1.call-start = ((), (), s32[]{:S(2)}) async-start(), calls=%async_computation.2 | async-start | bytes 3342336 | tf_op jit(solution)/shard_map/all_gather | solution.py:26
  105.0 68.5 %all-to-all-start.1 = ((bf16[16,2,24576]{2,1,0:T(2,128)(2,1)}), bf16[16,2,24576]{2,1,0:T(2,128)(2,1)}, u32[]{:S(2)}, u32[]{:S(2)}) async-start(bf16[16,2,24576]{2,1,0:T(2,128)(2,1)} %reshape.163), calls=%async_computation.1 | async-start | bytes 3145728 | tf_op jit(solution)/shard_map/all_to_all | solution.py:29
  113.2 174.8 %all-reduce.5.cloned.1.call-start = ((), (), s32[]{:S(2)}) async-start(), calls=%async_computation.3 | async-start | bytes 1048576 | tf_op jit(solution)/shard_map/psum | solution.py:13
  120.5 2.2 copy-start
  196.5 1.7 copy-start.1
  204.9 145.5 %all-reduce.7.cloned.1.call-start = ((), (), s32[]{:S(2)}) async-start(), calls=%async_computation.4 | async-start | bytes 1048576 | tf_op jit(solution)/shard_map/psum | solution.py:13
  288.0 157.9 %all-reduce.9.cloned.1.call-start = ((), (), s32[]{:S(2)}) async-start(), calls=%async_computation.5 | async-start | bytes 1048576 | tf_op jit(solution)/shard_map/psum | solution.py:13
  360.9 1.8 copy-start.2
  367.8 132.1 %all-reduce.11.cloned.1.call-start = ((), (), s32[]{:S(2)}) async-start(), calls=%async_computation.6 | async-start | bytes 1048576 | tf_op jit(solution)/shard_map/psum | solution.py:13
  507.8 5.2 copy-start.3
  507.8 5.2 copy-start.4
Sparse Core Ops, SparseCore 0:
  23.0 65.0 all-gather.1
  205.0 82.9 all-reduce.4
  290.4 51.8 all-reduce.6
  367.9 77.9 all-reduce.8
  448.1 51.7 all-reduce.10
where the time goes:
time: 524 us; the launch traced here: 522 us
  waiting for transfers between devices  272 us (52%)
  local copies, waits for them, and re-layouts  104 us (20%)
  other arithmetic  93.7 us (18%)
  matrix products  20.2 us (4%)
  starting transfers between devices  18.4 us (4%)
  between operations  13.5 us (3%)
    psum x4, waiting for transfers between devices, spread(): shard = lax.psum(shard, axis)  215 us
    another operation x4, other arithmetic, body(): jax.scipy.linalg.solve_triangular(mine, work[0], lower=True)  81.2 us
    all_to_all x1, waiting for transfers between devices, body(): lax.all_to_all(rhs, 'col', split_axis=2, concat_axis=3, tiled=True)  56.9 us
    unnamed x21, local copies, waits for them, and re-layouts  32.9 us
    another operation x27, local copies, waits for them, and re-layouts, body(): jax.scipy.linalg.solve_triangular(mine, work[0], lower=True)  25.7 us
    another operation x14, matrix products, body(): jax.scipy.linalg.solve_triangular(mine, work[0], lower=True)  11.6 us
  transfers between devices with their start and end apart: 7, of which 4 were waited for; matrix products, arithmetic and copies ran while one was open for 29% of the time, Pallas kernels for 0%

commit v1 on v0

--- a/solution.py
+++ b/solution.py
@@ -5,6 +5,13 @@
 from jax.sharding import PartitionSpec as P
 
 ROW = ("row_0", "row_1")
+
+
+def stacked_exchange(x, name, split, join):
+    size = lax.axis_size(name)
+    blocks = jnp.stack(jnp.split(x, size, axis=split), axis=0)
+    blocks = lax.all_to_all(blocks, name, split_axis=0, concat_axis=0)
+    return jnp.concatenate(blocks, axis=join)
 
 
 def spread(shard, axes, root):
@@ -26,14 +33,13 @@
     whole = lax.all_gather(lower, "col", axis=4, tiled=True)
     panels = whole[0]
     rows = panels.shape[0] * tile
-    rhs = lax.all_to_all(
+    rhs = stacked_exchange(
         reorder(
             lax.all_to_all(rhs, "col", split_axis=2, concat_axis=3, tiled=True), tile_map, tile
         ),
         "col",
-        split_axis=3,
-        concat_axis=2,
-        tiled=True,
+        3,
+        2,
     )
     work = rhs[0].astype(jnp.float32)
     identity = jnp.eye(tile, dtype=jnp.float32)

time: 524 us -> 531 us (1.013)
  waiting for transfers between devices: 272 us -> 307 us
  local copies, waits for them, and re-layouts: 104 us -> 75.6 us
    all_to_all x1, waiting for transfers between devices: 0.01 us -> 35.6 us  [stacked_exchange(): blocks = lax.all_to_all(blocks, name, split_axis=0, concat_axis=0)]
    unnamed x21 -> x37, local copies, waits for them, and re-layouts: 32.9 us -> 18.2 us
    all_to_all x2 -> x0, local copies, waits for them, and re-layouts: 11.2 us -> none  [the longest x1 9.68 us: body(): lax.all_to_all(reorder(lax.all_to_all(rhs, 'col', split_axis=2, concat_ax...]
    select_n x1 -> x0, local copies, waits for them, and re-layouts: 8.34 us -> none  [reorder(): return jnp.take(tiles, tile_map, axis=3).reshape(shape)]
  transfers between devices with their start and end apart: 7 -> 7, of which waited for: 4 -> 5; matrix products, arithmetic and copies ran while one was open for 29% -> 16% of each run, Pallas kernels for 0% -> 0%
where the time goes in v1:
time: 531 us; the launch traced here: 530 us
  waiting for transfers between devices  307 us (58%)
  other arithmetic  94.3 us (18%)
  local copies, waits for them, and re-layouts  75.6 us (14%)
  matrix products  21.3 us (4%)
  starting transfers between devices  18.1 us (3%)
  between operations  13.5 us (3%)
    psum x4, waiting for transfers between devices, spread(): shard = lax.psum(shard, axis)  215 us
    another operation x4, other arithmetic, body(): jax.scipy.linalg.solve_triangular(mine, work[0], lower=True)  81.4 us
    all_to_all x1, waiting for transfers between devices, body(): lax.all_to_all(rhs, 'col', split_axis=2, concat_axis=3, tiled=True)  56.9 us
    all_to_all x1, waiting for transfers between devices, stacked_exchange(): blocks = lax.all_to_all(blocks, name, split_axis=0, concat_axis=0)  35.6 us
    another operation x27, local copies, waits for them, and re-layouts, body(): jax.scipy.linalg.solve_triangular(mine, work[0], lower=True)  26.5 us
    unnamed x37, local copies, waits for them, and re-layouts  18.2 us
    another operation x14, matrix products, body(): jax.scipy.linalg.solve_triangular(mine, work[0], lower=True)  12.7 us
  transfers between devices with their start and end apart: 7, of which 5 were waited for; matrix products, arithmetic and copies ran while one was open for 16% of the time, Pallas kernels for 0%

profile of v1, /device:TPU:8, one launch (start us, length us, event | category | flops | bytes accessed | tf_op | source)
XLA Modules:
  0.0 530.1 jit_solution(9688891220978987260)
XLA Ops:
  6.5 4.1 copy.46
  10.6 9.4 %all-to-all-start = ((bf16[1,3,512,512]{3,1,0,2:T(4,128)(2,1)}), bf16[1,3,512,512]{3,1,0,2:T(4,128)(2,1)S(1)}, u32[]{:S(2)}, u32[]{:S(2)}) async-start(bf16[1,3,512,512]{3,1,0,2:T(4,128)(2,1)} %copy.46), calls=%async_computation | async-start | bytes 4194304 | tf_op jit(solution)/shard_map/all_to_all | solution.py:38
  20.1 0.9 copy.49
  21.2 56.9 %all-to-all-done = bf16[1,3,512,512]{3,1,0,2:T(4,128)(2,1)S(1)} async-done(((bf16[1,3,512,512]{3,1,0,2:T(4,128)(2,1)}), bf16[1,3,512,512]{3,1,0,2:T(4,128)(2,1)S(1)}, u32[]{:S(2)}, u32[]{:S(2)}) %all-to-all-start) | async-done | bytes 1572896 | tf_op jit(solution)/shard_map/all_to_all | solution.py:38
  78.1 1.3 copy-done.3
  79.4 4.0 gather_fusion
  83.4 2.3 copy.47
  85.6 2.6 gather.9
  98.8 8.1 %all-to-all-start.1 = ((bf16[16,1,3,32,512]{4,3,2,1,0:T(8,128)(2,1)}), bf16[16,1,3,32,512]{4,3,2,1,0:T(8,128)(2,1)S(1)}, u32[]{:S(2)}, u32[]{:S(2)}) async-start(bf16[16,1,3,32,512]{4,3,2,1,0:T(8,128)(2,1)} %fusion.36), calls=%async_computation.1 | async-start | bytes 3145728 | tf_op jit(solution)/shard_map/all_to_all | solution.py:13
  107.1 35.6 %all-to-all-done.1 = bf16[16,1,3,32,512]{4,3,2,1,0:T(8,128)(2,1)S(1)} async-done(((bf16[16,1,3,32,512]{4,3,2,1,0:T(8,128)(2,1)}), bf16[16,1,3,32,512]{4,3,2,1,0:T(8,128)(2,1)S(1)}, u32[]{:S(2)}, u32[]{:S(2)}) %all-to-all-start.1) | async-done | bytes 1572896 | tf_op jit(solution)/shard_map/all_to_all | solution.py:13
  143.2 1.6 copy-done
  144.8 1.1 slice.87
  145.9 7.0 %copy.50 = bf16[1,3,512,2,512]{4,2,3,1,0:T(8,128)(2,1)S(1)} copy(bf16[1,3,512,2,512]{2,3,1,0,4:T(2,128)(2,1)} %all-gather.2.cloned.1.call-done) | data formatting | bytes 6291456 | tf_op jit(solution)/shard_map/all_gather | solution.py:33
  152.9 2.0 fusion.3
  155.3 11.5 %while.5 = (s32[]{:T(128)}, f32[512,512]{1,0:T(8,128)}, s32[4,2]{0,1:T(2,128)S(1)}, f32[4,128,128]{2,1,0:T(8,128)S(1)}, s32[]{:T(128)}) while((s32[]{:T(128)}, f32[512,512]{1,0:T(8,128)}, s32[4,2]{0,1:T(2,128)S(1)}, f32[4,128,128]{2,1,0:T(8,128)S(1)}, s32[]{:T(128)}) %tuple.41), condition=%wide.while_cond.1, body=%wide.while_body.1.sunk | while | flops 2 | bytes 131189 | solution.py:51
  155.9 2.2 bitcast_dynamic-update-slice_fusion.4
  158.8 2.2 bitcast_dynamic-update-slice_fusion.4
  161.7 2.2 bitcast_dynamic-update-slice_fusion.4
  164.6 2.2 bitcast_dynamic-update-slice_fusion.4
  166.8 39.3 %custom-call.4 = f32[4,128,128]{1,2,0:T(8,128)S(1)} custom-call(f32[4,128,128]{2,1,0:T(8,128)S(1)} %get-tuple-element.32), custom_call_target="InvertDiagBlocksLowerTriangular" | custom-call | tf_op jit(solution)/shard_map/jit(_solve_triangular)/triangular_solve | solution.py:51
  206.1 1.4 fusion.30
  207.5 1.4 convolution_subtract_fusion.3
  209.3 1.3 convolution_subtract_fusion.2
  211.1 1.6 convolution_subtract_fusion.5
  213.0 0.9 fusion.16
  214.0 82.7 %all-reduce.5.cloned.1.call-done = bf16[512,512]{1,0:T(8,128)(2,1)} async-done(((bf16[512,512]{1,0:T(8,128)(2,1)}), bf16[512,512]{1,0:T(8,128)(2,1)}) %all-reduce.5.cloned.1.call-update) | async-done | bytes 524304 | tf_op jit(solution)/shard_map/psum | solution.py:20
  297.0 0.7 broadcast.88.clone.1
  297.7 14.3 %while.6 = (s32[]{:T(128)}, f32[512,512]{1,0:T(8,128)}, s32[4,2]{0,1:T(2,128)S(1)}, f32[4,128,128]{2,1,0:T(8,128)}, s32[]{:T(128)}) while((s32[]{:T(128)}, f32[512,512]{1,0:T(8,128)}, s32[4,2]{0,1:T(2,128)S(1)}, f32[4,128,128]{2,1,0:T(8,128)}, s32[]{:T(128)}) %tuple.57), condition=%wide.while_cond.1.clone, body=%wide.while_body.1.clone.sunk | while | flops 2 | bytes 132205 | solution.py:51
  298.4 2.9 bitcast_dynamic-update-slice_fusion.5
  302.0 2.9 bitcast_dynamic-update-slice_fusion.5
  305.6 2.9 bitcast_dynamic-update-slice_fusion.5
  309.2 2.9 bitcast_dynamic-update-slice_fusion.5
  312.1 2.2 copy.48
  314.3 40.1 %custom-call.5 = f32[4,128,128]{1,2,0:T(8,128)S(1)} custom-call(f32[4,128,128]{2,1,0:T(8,128)} %get-tuple-element.33), custom_call_target="InvertDiagBlocksLowerTriangular" | custom-call | tf_op jit(solution)/shard_map/jit(_solve_triangular)/triangular_solve | solution.py:51
  354.4 4.0 fusion.66
  358.4 4.3 convolution_bitcast_fusion.1
  362.7 3.6 copy.51
  366.2 2.6 sub.25
  369.4 1.3 convolution_subtract_fusion.1
  371.1 1.3 convolution_subtract_fusion
  372.9 1.6 convolution_subtract_fusion.4
  374.9 0.9 fusion.15
  375.8 78.1 %all-reduce.9.cloned.1.call-done = bf16[512,512]{1,0:T(8,128)(2,1)} async-done(((bf16[512,512]{1,0:T(8,128)(2,1)}), bf16[512,512]{1,0:T(8,128)(2,1)}) %all-reduce.9.cloned.1.call-update) | async-done | bytes 524304 | tf_op jit(solution)/shard_map/psum | solution.py:20
  453.9 54.0 %all-reduce.11.cloned.1.call-done = bf16[512,512]{1,0:T(8,128)(2,1)} async-done(((bf16[512,512]{1,0:T(8,128)(2,1)}), bf16[512,512]{1,0:T(8,128)(2,1)}) %all-reduce.11.cloned.1.call-update) | async-done | bytes 524304 | tf_op jit(solution)/shard_map/psum | solution.py:20
  507.9 4.3 convolution_bitcast_fusion
  512.1 3.6 copy.54
  515.8 5.2 fusion.1
  520.9 2.7 fusion.21
  (78 shorter events, 20.4 us)
Async XLA Ops:
  10.6 9.5 %copy-start.7 = (bf16[1,3,512,2,32]{2,4,3,1,0:T(8,128)(2,1)S(1)}, bf16[1,3,512,2,32]{2,4,3,1,0:T(8,128)(2,1)}, u32[]{:S(2)}) copy-start(bf16[1,3,512,2,32]{2,4,3,1,0:T(8,128)(2,1)} %param.7) | copy-start | bytes 589828
  10.6 10.4 %copy-start.8 = (s32[16]{0:T(128)S(1)}, s32[16]{0:T(128)}, u32[]{:S(2)}) copy-start(s32[16]{0:T(128)} %param.9) | copy-start | bytes 196
  10.6 67.4 %all-to-all-start = ((bf16[1,3,512,512]{3,1,0,2:T(4,128)(2,1)}), bf16[1,3,512,512]{3,1,0,2:T(4,128)(2,1)S(1)}, u32[]{:S(2)}, u32[]{:S(2)}) async-start(bf16[1,3,512,512]{3,1,0,2:T(4,128)(2,1)} %copy.46), calls=%async_computation | async-start | bytes 4194304 | tf_op jit(solution)/shard_map/all_to_all | solution.py:38
  20.1 125.8 %all-gather.2.cloned.1.call-start = ((), (), s32[]{:S(2)}) async-start(), calls=%async_computation.2 | async-start | bytes 3342336 | tf_op jit(solution)/shard_map/all_gather | solution.py:33
  78.1 1.3 copy-start.3
  98.8 44.0 %all-to-all-start.1 = ((bf16[16,1,3,32,512]{4,3,2,1,0:T(8,128)(2,1)}), bf16[16,1,3,32,512]{4,3,2,1,0:T(8,128)(2,1)S(1)}, u32[]{:S(2)}, u32[]{:S(2)}) async-start(bf16[16,1,3,32,512]{4,3,2,1,0:T(8,128)(2,1)} %fusion.36), calls=%async_computation.1 | async-start | bytes 3145728 | tf_op jit(solution)/shard_map/all_to_all | solution.py:13
  106.9 189.8 %all-reduce.5.cloned.1.call-start = ((), (), s32[]{:S(2)}) async-start(), calls=%async_computation.3 | async-start | bytes 1048576 | tf_op jit(solution)/shard_map/psum | solution.py:20
  143.2 1.7 copy-start
  152.9 2.4 copy-start.1
  155.3 54.0 %copy-start.4 = (f32[1,1,16,32,512]{4,3,1,0,2:T(8,128)S(1)}, f32[1,1,16,32,512]{4,3,1,0,2:T(8,128)}, u32[]{:S(2)}) copy-start(f32[1,1,16,32,512]{4,3,1,0,2:T(8,128)} %slice.87) | copy-start | bytes 3145732
  214.0 144.4 %all-reduce.7.cloned.1.call-start = ((), (), s32[]{:S(2)}) async-start(), calls=%async_computation.4 | async-start | bytes 1048576 | tf_op jit(solution)/shard_map/psum | solution.py:20
  296.7 157.2 %all-reduce.9.cloned.1.call-start = ((), (), s32[]{:S(2)}) async-start(), calls=%async_computation.5 | async-start | bytes 1048576 | tf_op jit(solution)/shard_map/psum | solution.py:20
  368.9 1.8 copy-start.2
  375.8 132.1 %all-reduce.11.cloned.1.call-start = ((), (), s32[]{:S(2)}) async-start(), calls=%async_computation.6 | async-start | bytes 1048576 | tf_op jit(solution)/shard_map/psum | solution.py:20
  515.7 5.2 copy-start.5
  515.7 5.2 copy-start.6
Sparse Core Ops, SparseCore 0:
  23.0 65.0 all-gather.1
  214.1 82.5 all-reduce.4
  299.1 52.2 all-reduce.6
  375.9 77.9 all-reduce.8
  456.1 51.7 all-reduce.10
